TPU v7x, 256 devices: a whole 4x4x8 slice. The times are simulated.
256 devices in a mesh: lb: 8 (over z), rb: 16 (over x, y), wa: 2 (over core).
Axes of the slice: x: 4, y: 4, z: 8, core: 2. Of those that a mesh axis runs over, the one named last changes fastest.
Arguments:
- initial_guess: bfloat16 [8192, 4, 128], P(('lb', 'rb')), may hold values from -6 to 6
- left_environment: bfloat16 [8, 8, 16, 64, 8192], P('wa', None, 'rb', None, 'lb'), may hold values from -12 to 12, as said below
- right_environment: bfloat16 [128, 8, 128], replicated, may hold values from -12 to 12, as said below
- operator_blocks: float32 [16, 4, 4], replicated, may hold values from -4 to 4
- operator_pairs: int32 [16, 2], replicated, may hold values from 0 to 7
Outputs:
- ritz_vector: float32 [8192, 4, 128], P(('lb', 'rb'))
- residual: float32 [8192, 4, 128], P(('lb', 'rb'))
Inputs may be any that keep to these rules, and one draw needn't show every extreme that they name: `operator_pairs`: each row names the left and the right MPO index of one operator block; blocks with the same pair add. `left_environment`: for each MPO index the [8192, 8192] matrix is symmetric. `right_environment`: for each MPO index the matrix over the two right bond states is symmetric.
All inputs are finite; a program needn't handle non-finite values.
Results may differ from a plain program's by a relative error of at most 0.014.
Values may be sent and summed in bfloat16 or wider, within the bound.
No kernel may reach another device: no remote copies, remote signals or barrier semaphores. Data moves between devices by JAX's collectives and lax.ppermute only.
A program may use at most 128 MiB of HBM per device.

v0:
```python
import functools

import jax
import jax.numpy as jnp
from jax import lax
from jax.sharding import Mesh
from jax.sharding import PartitionSpec as P

ITERS = 3
SWEEPS = 8
RB = ("rb_0", "rb_1")
LB_RB = ("lb", "rb_0", "rb_1")


highest = lax.Precision.HIGHEST
epsilon = 1e-06


def sent_to_all(x, axis):
    size = lax.axis_size(axis)
    return lax.all_to_all(jnp.broadcast_to(x[None], (size, *x.shape)), axis, 0, 0, tiled=True)


def taken_together(x, axis):
    return sent_to_all(x, axis).sum(axis=0)


def in_order(tiles, dim):
    lengths = list(tiles.shape[1:])
    lengths[dim] *= tiles.shape[0]
    return jnp.moveaxis(tiles, 0, dim).reshape(lengths)


def gathered_copies(x, axis, dim):
    return in_order(sent_to_all(x, axis), dim)


def in_blocks(x, dim, size):
    lengths = x.shape
    tiles = x.reshape(*lengths[:dim], size, lengths[dim] // size, *lengths[dim + 1 :])
    return jnp.moveaxis(tiles, dim, 0)


def summed_on_arrival(x, axis, dim):
    tiles = in_blocks(x, dim, lax.axis_size(axis))
    arrived = lax.all_to_all(tiles, axis, split_axis=0, concat_axis=0, tiled=True)
    return arrived.sum(axis=0)


def by_axis(x, axes):
    return functools.reduce(lax.psum, axes, x)


def lowest_pair(matrix):
    matrix_order = matrix.shape[0]
    vectors = jnp.eye(matrix_order, dtype=jnp.float32)
    positions = jnp.arange(matrix_order, dtype=jnp.int32)
    for rounds in range(SWEEPS):
        for first_row in range(matrix_order):
            for second_row in range(first_row + 1, matrix_order):
                rotation_angle = 0.5 * jnp.arctan2(
                    2.0 * matrix[first_row, second_row],
                    matrix[second_row, second_row] - matrix[first_row, first_row],
                )
                cosine = jnp.cos(rotation_angle)
                sine_value = jnp.sin(rotation_angle)
                first_mask = positions == first_row
                second_mask = positions == second_row
                first_col = matrix[:, first_row : first_row + 1]
                second_col = matrix[:, second_row : second_row + 1]
                matrix = jnp.where(
                    first_mask[None, :],
                    cosine * first_col - sine_value * second_col,
                    jnp.where(
                        second_mask[None, :], sine_value * first_col + cosine * second_col, matrix
                    ),
                )
                first_line = matrix[first_row : first_row + 1, :]
                second_line = matrix[second_row : second_row + 1, :]
                matrix = jnp.where(
                    first_mask[:, None],
                    cosine * first_line - sine_value * second_line,
                    jnp.where(
                        second_mask[:, None], sine_value * first_line + cosine * second_line, matrix
                    ),
                )
                first_vec = vectors[:, first_row : first_row + 1]
                second_vec = vectors[:, second_row : second_row + 1]
                vectors = jnp.where(
                    first_mask[None, :],
                    cosine * first_vec - sine_value * second_vec,
                    jnp.where(
                        second_mask[None, :], sine_value * first_vec + cosine * second_vec, vectors
                    ),
                )
    values = jnp.diagonal(matrix)
    chosen = (positions == jnp.argmin(values)).astype(jnp.float32)
    ritz_value = jnp.sum(values * chosen)
    weights = jnp.sum(vectors * chosen[None, :], axis=1)
    weights = jnp.where(weights[0] < 0.0, -weights, weights)
    return (ritz_value, weights)


def dense_operator(operator_blocks, operator_pairs, levels):
    symmetric = 0.5 * (operator_blocks + jnp.swapaxes(operator_blocks, 1, 2))
    indices = jnp.arange(levels, dtype=jnp.int32)
    left_hot = (operator_pairs[:, 0:1] == indices[None, :]).astype(jnp.float32)
    right_hot = (operator_pairs[:, 1:2] == indices[None, :]).astype(jnp.float32)
    return jnp.einsum("nw,nv,nts->wvts", left_hot, right_hot, symmetric, precision=highest)


def contract_right(vector_rows, right_matrix, local_operator):
    row_count, physical, window = vector_rows.shape
    levels = local_operator.shape[1]
    mixed = jnp.dot(
        vector_rows.reshape(row_count * physical, window),
        right_matrix,
        preferred_element_type=jnp.float32,
    )
    mixed = mixed.reshape(row_count, physical, levels, window)
    return jnp.einsum("kvts,nsvb->kntb", local_operator, mixed, precision=highest).astype(
        jnp.bfloat16
    )


def combine(members, weights):
    total = weights[0] * members[0]
    for member_index in range(1, len(members)):
        total = total + weights[member_index] * members[member_index]
    return total


def per_device(initial_guess, left_environment, right_environment, operator_blocks, operator_pairs):
    own_rows, physical, window = initial_guess.shape
    levels = right_environment.shape[1]
    local_levels = left_environment.shape[0]
    block_rows = left_environment.shape[1] * left_environment.shape[3]
    contracted = left_environment.shape[4]
    total_count = own_rows * physical * window * lax.axis_size("lb") * lax.axis_size(RB)
    left_index = lax.axis_index("lb")
    right_index = lax.axis_index(RB)
    level_index = lax.axis_index("wa")
    operator = dense_operator(operator_blocks, operator_pairs, levels)
    local_operator = lax.dynamic_slice_in_dim(operator, level_index * local_levels, local_levels, 0)
    left_matrix = left_environment.reshape(local_levels, block_rows, contracted)
    right_matrix = right_environment.reshape(window, levels * window)
    own_block = lax.dynamic_slice_in_dim(left_environment, left_index, 1, 1)
    own_block = lax.dynamic_slice_in_dim(own_block, right_index * own_rows, own_rows, 4)
    own_block = own_block.reshape(local_levels, own_rows, own_rows)
    left_diag = jnp.diagonal(own_block, axis1=1, axis2=2).astype(jnp.float32)
    operator_diag = jnp.diagonal(local_operator, axis1=2, axis2=3)
    right_diag = jnp.diagonal(right_environment, axis1=0, axis2=2).astype(jnp.float32)
    diagonal_part = jnp.einsum(
        "kr,kvs,vb->rsb", left_diag, operator_diag, right_diag, precision=highest
    )
    diagonal_values = taken_together(diagonal_part, "wa")

    def contract_piece(shard_rows):
        return contract_right(shard_rows, right_matrix, local_operator)

    def apply_hamiltonian(vector):
        vector_bf = vector.astype(jnp.bfloat16)
        inner_terms = contract_piece(gathered_copies(vector_bf, RB, 0))
        partial_value = summed_on_arrival(
            jnp.einsum(
                "kma,katb->mtb", left_matrix, inner_terms, preferred_element_type=jnp.float32
            ),
            "lb",
            0,
        )
        return taken_together(partial_value, "wa")

    def subspace_entries(members, image):
        local_sums = jnp.stack([jnp.sum(member * image) for member in members])
        return by_axis(local_sums, LB_RB) / total_count

    start_vector = initial_guess.astype(jnp.float32)
    start_norm = by_axis(jnp.sum(start_vector * start_vector), LB_RB) / total_count
    basis = [start_vector * lax.rsqrt(start_norm + epsilon)]
    images = [apply_hamiltonian(basis[0])]
    subspace = jnp.zeros((ITERS + 1, ITERS + 1), jnp.float32)
    subspace = subspace.at[0, 0].set(subspace_entries(basis, images[0])[0])
    for step_index in range(ITERS):
        filled = step_index + 1
        ritz_value, weights = lowest_pair(subspace[:filled, :filled])
        ritz_now = combine(basis, weights)
        residual_now = combine(images, weights) - ritz_value * ritz_now
        correction = residual_now / (jnp.abs(diagonal_values - ritz_value) + 1.0)
        local_correlations = jnp.stack([jnp.sum(member * correction) for member in basis])
        correlation_sums, square_sum = (
            by_axis(local_correlations, LB_RB),
            by_axis(jnp.sum(correction * correction), LB_RB),
        )
        correlation_values = correlation_sums / total_count
        correction = correction - combine(basis, correlation_values)
        squared = square_sum / total_count - jnp.sum(correlation_values * correlation_values)
        new_vector = correction * lax.rsqrt(squared + epsilon)
        new_image = apply_hamiltonian(new_vector)
        basis.append(new_vector)
        images.append(new_image)
        row_values = subspace_entries(basis, new_image)
        subspace = (
            subspace.at[filled, : filled + 1]
            .set(row_values)
            .at[: filled + 1, filled]
            .set(row_values)
        )
    ritz_value, weights = lowest_pair(subspace)
    ritz_vector = combine(basis, weights)
    residual = combine(images, weights) - ritz_value * ritz_vector
    return (ritz_vector, residual)


def solution(mesh):
    split = Mesh(
        mesh.devices.reshape(mesh.shape["lb"], 4, 4, mesh.shape["wa"]), ("lb", "rb_0", "rb_1", "wa")
    )
    in_specs = (P(LB_RB, None, None), P("wa", None, RB, None, "lb"), P(), P(), P())
    out_specs = (P(LB_RB, None, None), P(LB_RB, None, None))
    return jax.shard_map(
        per_device, mesh=split, in_specs=in_specs, out_specs=out_specs, check_vma=False
    )
```

profile of v0, /device:TPU:8, one launch (start us, length us, event | category | flops | bytes accessed | tf_op | source)
XLA Modules:
  0.0 920.6 jit_solution(16153142734862492179)
XLA Ops:
  2.1 20.6 %psum.231 = f32[]{:T(128)} all-reduce(f32[]{:T(128)} %fusion.93), channel_id=1, replica_groups=mesh['lb'=8,'rb_0'=4,'rb_1'=4,'wa'=2] {'lb'}, use_global_device_ids=true, to_apply=%region_1.2 | all-reduce | flops 1 | bytes 8 | tf_op jit(solution)/shard_map/psum | solution.py:51
  22.7 11.1 %psum.232 = f32[]{:T(128)} all-reduce(f32[]{:T(128)} %psum.231), channel_id=1, replica_groups=mesh['lb'=8,'rb_0'=4,'rb_1'=4,'wa'=2] {'rb_0'}, use_global_device_ids=true, to_apply=%region_2.3 | all-reduce | flops 1 | bytes 8 | tf_op jit(solution)/shard_map/psum | solution.py:51
  33.8 9.3 %psum.233 = f32[]{:T(128)} all-reduce(f32[]{:T(128)} %psum.232), channel_id=1, replica_groups=mesh['lb'=8,'rb_0'=4,'rb_1'=4,'wa'=2] {'rb_1'}, use_global_device_ids=true, to_apply=%region_3.4 | all-reduce | flops 1 | bytes 8 | tf_op jit(solution)/shard_map/psum | solution.py:51
  65.9 29.3 %fusion.24 = bf16[4,1024,4,128]{3,2,0,1:T(4,128)(2,1)S(1)} fusion(f32[1024,4,8,128,1]{3,0,2,1,4:T(8,128)S(1)} %convolution_bitcast_fusion.3, f32[4,8,4,4]{1,2,3,0:T(4,128)S(1)} %copy.123), kind=kOutput, calls=%fused_computation.30 | convolution fusion | flops 807403520 | bytes 20973568 | tf_op jit(solution)/shard_map/kvts,nsvb->kntb/dot_general | solution.py:121
  111.7 11.8 %all-to-all-done.1 = f32[8,64,4,128]{3,1,2,0:T(8,128)S(1)} async-done(((f32[8,64,4,128]{3,1,2,0:T(8,128)}), f32[8,64,4,128]{3,1,2,0:T(8,128)S(1)}, u32[]{:S(2)}, u32[]{:S(2)}) %all-to-all-start.1) | async-done | bytes 1048608 | tf_op jit(solution)/shard_map/all_to_all | solution.py:46
  128.2 14.8 %psum.234 = f32[1]{0:T(128)} all-reduce(f32[1]{0:T(128)} %bitcast.24), channel_id=1, replica_groups=mesh['lb'=8,'rb_0'=4,'rb_1'=4,'wa'=2] {'lb'}, use_global_device_ids=true, to_apply=%region_7.8 | all-reduce | flops 1 | bytes 8 | tf_op jit(solution)/shard_map/psum | solution.py:51
  147.2 9.6 %psum.235 = f32[1]{0:T(128)} all-reduce(f32[1]{0:T(128)} %psum.234), channel_id=1, replica_groups=mesh['lb'=8,'rb_0'=4,'rb_1'=4,'wa'=2] {'rb_0'}, use_global_device_ids=true, to_apply=%region_8.9 | all-reduce | flops 1 | bytes 8 | tf_op jit(solution)/shard_map/psum | solution.py:51
  156.8 9.8 %psum.236 = f32[1]{0:T(128)} all-reduce(f32[1]{0:T(128)} %psum.235), channel_id=1, replica_groups=mesh['lb'=8,'rb_0'=4,'rb_1'=4,'wa'=2] {'rb_1'}, use_global_device_ids=true, to_apply=%region_9.10 | all-reduce | flops 1 | bytes 8 | tf_op jit(solution)/shard_map/psum | solution.py:51
  167.9 16.9 %all-reduce.3 = (f32[]{:T(128)}, f32[1]{0:T(128)}) all-reduce(f32[]{:T(128)} %get-tuple-element.111, f32[1]{0:T(128)} %bitcast.36), channel_id=1, replica_groups=mesh['lb'=8,'rb_0'=4,'rb_1'=4,'wa'=2] {'lb'}, use_global_device_ids=true, to_apply=%region_16.17 | all-reduce | flops 2 | bytes 16 | tf_op jit(solution)/shard_map/psum | solution.py:51
  184.7 9.2 all-reduce.9
  193.9 9.3 %all-reduce.6 = (f32[]{:T(128)}, f32[1]{0:T(128)}) all-reduce(f32[]{:T(128)} %get-tuple-element.288, f32[1]{0:T(128)} %get-tuple-element.289), channel_id=1, replica_groups=mesh['lb'=8,'rb_0'=4,'rb_1'=4,'wa'=2] {'rb_1'}, use_global_device_ids=true, to_apply=%region_18.19 | all-reduce | flops 2 | bytes 16 | tf_op jit(solution)/shard_map/psum | solution.py:51
  206.2 16.6 %all_to_all.66 = bf16[16,64,4,128]{3,1,2,0:T(8,128)(2,1)S(1)} all-to-all(bf16[16,64,4,128]{3,1,2,0:T(8,128)(2,1)S(1)} %broadcast_in_dim.6367), channel_id=1, replica_groups=mesh['lb'=8,'rb_0'=4,'rb_1'=4,'wa'=2] {'rb_0','rb_1'}, dimensions={0} | all-to-all | bytes 2097152 | tf_op jit(solution)/shard_map/all_to_all | solution.py:21
  225.2 29.5 %fusion.27 = bf16[4,1024,4,128]{3,2,0,1:T(4,128)(2,1)S(1)} fusion(f32[1024,4,8,128,1]{3,0,2,1,4:T(8,128)S(1)} %convolution_bitcast_fusion.2, f32[4,8,4,4]{1,2,3,0:T(4,128)S(1)} %copy.123), kind=kOutput, calls=%fused_computation.31 | convolution fusion | flops 807403520 | bytes 20973568 | tf_op jit(solution)/shard_map/kvts,nsvb->kntb/dot_general | solution.py:121
  263.2 18.3 %all-to-all-done.5 = f32[8,64,4,128]{3,1,2,0:T(8,128)S(1)} async-done(((f32[8,64,4,128]{3,1,2,0:T(8,128)}), f32[8,64,4,128]{3,1,2,0:T(8,128)S(1)}, u32[]{:S(2)}, u32[]{:S(2)}) %all-to-all-start.5) | async-done | bytes 1048608 | tf_op jit(solution)/shard_map/all_to_all | solution.py:46
  287.7 14.7 %psum.243 = f32[2]{0:T(128)S(1)} all-reduce(f32[2]{0:T(128)S(1)} %pad_maximum_fusion), channel_id=1, replica_groups=mesh['lb'=8,'rb_0'=4,'rb_1'=4,'wa'=2] {'lb'}, use_global_device_ids=true, to_apply=%region_23.24 | all-reduce | flops 2 | bytes 16 | tf_op jit(solution)/shard_map/psum | solution.py:51
  311.2 9.2 psum.245
  355.8 16.3 %all-reduce.2 = (f32[]{:T(128)}, f32[2]{0:T(128)S(1)}) all-reduce(f32[]{:T(128)} %get-tuple-element.106, f32[2]{0:T(128)S(1)} %pad_maximum_fusion.1), channel_id=1, replica_groups=mesh['lb'=8,'rb_0'=4,'rb_1'=4,'wa'=2] {'lb'}, use_global_device_ids=true, to_apply=%region_35.36 | all-reduce | flops 3 | bytes 24 | tf_op jit(solution)/shard_map/psum | solution.py:51
  372.1 9.3 %all-reduce.8 = (f32[]{:T(128)}, f32[2]{0:T(128)S(1)}) all-reduce(f32[]{:T(128)} %get-tuple-element.274, f32[2]{0:T(128)S(1)} %get-tuple-element.275), channel_id=1, replica_groups=mesh['lb'=8,'rb_0'=4,'rb_1'=4,'wa'=2] {'rb_0'}, use_global_device_ids=true, to_apply=%region_36.37 | all-reduce | flops 3 | bytes 24 | tf_op jit(solution)/shard_map/psum | solution.py:51
  381.3 9.1 all-reduce.5
  394.5 17.2 %all_to_all.68 = bf16[16,64,4,128]{3,1,2,0:T(8,128)(2,1)S(1)} all-to-all(bf16[16,64,4,128]{3,1,2,0:T(8,128)(2,1)S(1)} %broadcast_in_dim.6469), channel_id=1, replica_groups=mesh['lb'=8,'rb_0'=4,'rb_1'=4,'wa'=2] {'rb_0','rb_1'}, dimensions={0} | all-to-all | bytes 2097152 | tf_op jit(solution)/shard_map/all_to_all | solution.py:21
  414.2 29.6 %fusion.30 = bf16[4,1024,4,128]{3,2,0,1:T(4,128)(2,1)S(1)} fusion(f32[1024,4,8,128,1]{3,0,2,1,4:T(8,128)S(1)} %convolution_bitcast_fusion.1, f32[4,8,4,4]{1,2,3,0:T(4,128)S(1)} %copy.123), kind=kOutput, calls=%fused_computation.32 | convolution fusion | flops 807403520 | bytes 20973568 | tf_op jit(solution)/shard_map/kvts,nsvb->kntb/dot_general | solution.py:121
  452.9 17.6 %all-to-all-done.8 = f32[8,64,4,128]{3,1,2,0:T(8,128)S(1)} async-done(((f32[8,64,4,128]{3,1,2,0:T(8,128)}), f32[8,64,4,128]{3,1,2,0:T(8,128)S(1)}, u32[]{:S(2)}, u32[]{:S(2)}) %all-to-all-start.8) | async-done | bytes 1048608 | tf_op jit(solution)/shard_map/all_to_all | solution.py:46
  477.4 14.7 %psum.252 = f32[3]{0:T(128)S(1)} all-reduce(f32[3]{0:T(128)S(1)} %pad_maximum_fusion.2), channel_id=1, replica_groups=mesh['lb'=8,'rb_0'=4,'rb_1'=4,'wa'=2] {'lb'}, use_global_device_ids=true, to_apply=%region_44.45 | all-reduce | flops 3 | bytes 24 | tf_op jit(solution)/shard_map/psum | solution.py:51
  500.9 9.2 psum.254
  601.0 16.3 %all-reduce.1 = (f32[]{:T(128)}, f32[3]{0:T(128)S(1)}) all-reduce(f32[]{:T(128)} %get-tuple-element.99, f32[3]{0:T(128)S(1)} %pad_maximum_fusion.3), channel_id=1, replica_groups=mesh['lb'=8,'rb_0'=4,'rb_1'=4,'wa'=2] {'lb'}, use_global_device_ids=true, to_apply=%region_58.59 | all-reduce | flops 4 | bytes 32 | tf_op jit(solution)/shard_map/psum | solution.py:51
  617.3 9.2 %all-reduce.7 = (f32[]{:T(128)}, f32[3]{0:T(128)S(1)}) all-reduce(f32[]{:T(128)} %get-tuple-element.272, f32[3]{0:T(128)S(1)} %get-tuple-element.273), channel_id=1, replica_groups=mesh['lb'=8,'rb_0'=4,'rb_1'=4,'wa'=2] {'rb_0'}, use_global_device_ids=true, to_apply=%region_59.60 | all-reduce | flops 4 | bytes 32 | tf_op jit(solution)/shard_map/psum | solution.py:51
  626.5 8.9 all-reduce.4
  640.3 17.1 %all_to_all.70 = bf16[16,64,4,128]{3,1,2,0:T(8,128)(2,1)S(1)} all-to-all(bf16[16,64,4,128]{3,1,2,0:T(8,128)(2,1)S(1)} %broadcast_in_dim.6765), channel_id=1, replica_groups=mesh['lb'=8,'rb_0'=4,'rb_1'=4,'wa'=2] {'rb_0','rb_1'}, dimensions={0} | all-to-all | bytes 2097152 | tf_op jit(solution)/shard_map/all_to_all | solution.py:21
  659.9 29.1 %fusion.33 = bf16[4,1024,4,128]{3,2,0,1:T(4,128)(2,1)S(1)} fusion(f32[1024,4,8,128,1]{3,0,2,1,4:T(8,128)S(1)} %convolution_bitcast_fusion, f32[4,8,4,4]{1,2,3,0:T(4,128)S(1)} %copy.123), kind=kOutput, calls=%fused_computation.33 | convolution fusion | flops 807403520 | bytes 20973568 | tf_op jit(solution)/shard_map/kvts,nsvb->kntb/dot_general | solution.py:121
  692.3 22.3 %all_to_all.71 = f32[8,64,4,128]{3,1,2,0:T(8,128)S(1)} all-to-all(f32[8,64,4,128]{3,1,2,0:T(8,128)S(1)} %copy.154), channel_id=1, replica_groups=mesh['lb'=8,'rb_0'=4,'rb_1'=4,'wa'=2] {'lb'}, dimensions={0} | all-to-all | bytes 2097152 | tf_op jit(solution)/shard_map/all_to_all | solution.py:46
  722.0 14.7 %psum.261 = f32[4]{0:T(128)S(1)} all-reduce(f32[4]{0:T(128)S(1)} %pad_maximum_fusion.4), channel_id=1, replica_groups=mesh['lb'=8,'rb_0'=4,'rb_1'=4,'wa'=2] {'lb'}, use_global_device_ids=true, to_apply=%region_68.69 | all-reduce | flops 4 | bytes 32 | tf_op jit(solution)/shard_map/psum | solution.py:51
  745.6 9.2 psum.263
  (639 shorter events, 245.1 us)
Async XLA Ops:
  45.9 17.6 %all-to-all-start = ((bf16[16,64,4,128]{3,1,2,0:T(8,128)(2,1)}), bf16[16,64,4,128]{3,1,2,0:T(8,128)(2,1)S(1)}, u32[]{:S(2)}, u32[]{:S(2)}) async-start(bf16[16,64,4,128]{3,1,2,0:T(8,128)(2,1)} %broadcast_in_dim.6364), calls=%async_computation | async-start | bytes 2097152 | tf_op jit(solution)/shard_map/all_to_all | solution.py:21
  65.9 29.3 %copy-start.2 = (bf16[4,8,1,64,1024]{4,3,2,1,0:T(8,128)(2,1)S(1)}, bf16[4,8,1,64,1024]{4,3,2,1,0:T(8,128)(2,1)}, u32[]{:S(2)}) copy-start(bf16[4,8,1,64,1024]{4,3,2,1,0:T(8,128)(2,1)} %param.20) | copy-start | bytes 12582916
  98.0 5.2 copy-start.1
  99.4 24.1 %all-to-all-start.1 = ((f32[8,64,4,128]{3,1,2,0:T(8,128)}), f32[8,64,4,128]{3,1,2,0:T(8,128)S(1)}, u32[]{:S(2)}, u32[]{:S(2)}) async-start(f32[8,64,4,128]{3,1,2,0:T(8,128)} %copy.126), calls=%async_computation.1 | async-start | bytes 2097152 | tf_op jit(solution)/shard_map/all_to_all | solution.py:46
  103.3 24.3 %copy-start = (bf16[64,4,128]{2,1,0:T(4,128)(2,1)S(1)}, bf16[64,4,128]{2,1,0:T(4,128)(2,1)}, u32[]{:S(2)}) copy-start(bf16[64,4,128]{2,1,0:T(4,128)(2,1)} %param.19) | copy-start | bytes 196612
  143.7 13.0 %all-to-all-start.3 = ((f32[2,64,4,128]{3,1,2,0:T(8,128)}), f32[2,64,4,128]{3,1,2,0:T(8,128)S(1)}, u32[]{:S(2)}, u32[]{:S(2)}) async-start(f32[2,64,4,128]{3,1,2,0:T(8,128)} %broadcast_in_dim.6366), calls=%async_computation.3 | async-start | bytes 524288 | tf_op jit(solution)/shard_map/all_to_all | solution.py:21
  225.2 29.5 %copy-start.3 = (bf16[4,8,1,64,1024]{4,3,2,1,0:T(8,128)(2,1)S(1)}, bf16[4,8,1,64,1024]{4,3,2,1,0:T(8,128)(2,1)}, u32[]{:S(2)}) copy-start(bf16[4,8,1,64,1024]{4,3,2,1,0:T(8,128)(2,1)} %param.20) | copy-start | bytes 12582916
  258.9 22.6 %all-to-all-start.5 = ((f32[8,64,4,128]{3,1,2,0:T(8,128)}), f32[8,64,4,128]{3,1,2,0:T(8,128)S(1)}, u32[]{:S(2)}, u32[]{:S(2)}) async-start(f32[8,64,4,128]{3,1,2,0:T(8,128)} %copy.138), calls=%async_computation.5 | async-start | bytes 2097152 | tf_op jit(solution)/shard_map/all_to_all | solution.py:46
  414.2 29.6 %copy-start.4 = (bf16[4,8,1,64,1024]{4,3,2,1,0:T(8,128)(2,1)S(1)}, bf16[4,8,1,64,1024]{4,3,2,1,0:T(8,128)(2,1)}, u32[]{:S(2)}) copy-start(bf16[4,8,1,64,1024]{4,3,2,1,0:T(8,128)(2,1)} %param.20) | copy-start | bytes 12582916
  446.5 5.7 copy-start.6
  447.9 22.6 %all-to-all-start.8 = ((f32[8,64,4,128]{3,1,2,0:T(8,128)}), f32[8,64,4,128]{3,1,2,0:T(8,128)S(1)}, u32[]{:S(2)}, u32[]{:S(2)}) async-start(f32[8,64,4,128]{3,1,2,0:T(8,128)} %copy.146), calls=%async_computation.8 | async-start | bytes 2097152 | tf_op jit(solution)/shard_map/all_to_all | solution.py:46
  659.9 29.2 %copy-start.5 = (bf16[4,8,1,64,1024]{4,3,2,1,0:T(8,128)(2,1)S(1)}, bf16[4,8,1,64,1024]{4,3,2,1,0:T(8,128)(2,1)}, u32[]{:S(2)}) copy-start(bf16[4,8,1,64,1024]{4,3,2,1,0:T(8,128)(2,1)} %param.20) | copy-start | bytes 12582916
where the time goes:
time: 928 us; the launch traced here: 921 us
  blocking collectives  367 us (40%)
  between operations  186 us (20%)
  matrix products  140 us (15%)
  local copies, waits for them, and re-layouts  83.2 us (9%)
  other arithmetic  69 us (7%)
  waiting for transfers between devices  56 us (6%)
  starting transfers between devices  20.3 us (2%)
    psum x24, blocking collectives, by_axis(): return functools.reduce(lax.psum, axes, x)  278 us
    dot_general x4, matrix products, contract_right(): jnp.einsum('kvts,nsvb->kntb', local_operator, mixed, precision=highest)  118 us
    all_to_all x7, blocking collectives, sent_to_all(): lax.all_to_all(jnp.broadcast_to(x[None], (size, *x.shape)), axis, 0, 0, t...  66.7 us
    slice x80, local copies, waits for them, and re-layouts, lowest_pair(): matrix[first_row, first_row]  53.7 us
    all_to_all x3, waiting for transfers between devices, summed_on_arrival(): lax.all_to_all(tiles, axis, split_axis=0, concat_axis=0, tiled=True)  47.7 us
    all_to_all x1, blocking collectives, summed_on_arrival(): lax.all_to_all(tiles, axis, split_axis=0, concat_axis=0, tiled=True)  22.3 us
  transfers between devices with their start and end apart: 5, of which 4 were waited for; matrix products, arithmetic and copies ran while one was open for 2% of the time, Pallas kernels for 0%

commit v1 on v0

v1 whole, which is shorter than its diff:
```python
import functools

import jax
import jax.numpy as jnp
from jax import lax
from jax.experimental import pallas as pl
from jax.experimental.pallas import tpu as pltpu
from jax.sharding import Mesh
from jax.sharding import PartitionSpec as P

ITERS = 3
SWEEPS = 8
S = 4
LANES = 128
HALF = 32
TILE = S * HALF
EXT = 16
N_LB = 8
N_RB = 16
RB = ("rb_0", "rb_1")
LB_RB = ("lb", "rb_0", "rb_1")
LB_WA = ("lb", "wa")
RB_WA = ("rb_0", "rb_1", "wa")
SEGMENTS = ((0, N_RB, 0), (N_RB, N_RB, 1), (2 * N_RB, N_LB, 0), (2 * N_RB + N_LB, N_LB, 1))
BLOCKS = 2 * (N_RB + N_LB)

highest = lax.Precision.HIGHEST
epsilon = 1e-06
f32 = jnp.float32
bf16 = jnp.bfloat16


def rotate(matrix, vectors, order, p, q):
    y = 2.0 * matrix[p, q]
    x = matrix[q, q] - matrix[p, p]
    large = jnp.maximum(jnp.abs(x), jnp.abs(y))
    zero = large == 0.0
    scale = 1.0 / jnp.where(zero, 1.0, large)
    xs, ys = x * scale, y * scale
    inverse = lax.rsqrt(jnp.where(zero, 1.0, xs * xs + ys * ys))
    half = 0.5 + 0.5 * jnp.abs(xs) * inverse
    root = lax.rsqrt(half)
    big = half * root
    small = 0.5 * jnp.abs(ys) * inverse * root
    ahead = x >= 0.0
    cosine = jnp.where(zero, 1.0, jnp.where(ahead, big, small))
    sine = jnp.where(ahead, small, big)
    sine = jnp.where(zero, 0.0, jnp.where(y < 0.0, -sine, sine))
    at = lambda a, b: (a, b) if a <= b else (b, a)
    pp, qq, pq = matrix[p, p], matrix[q, q], matrix[p, q]
    cc, ss, cs = cosine * cosine, sine * sine, cosine * sine
    new = dict(matrix)
    new[p, p] = cc * pp - 2.0 * cs * pq + ss * qq
    new[q, q] = ss * pp + 2.0 * cs * pq + cc * qq
    new[p, q] = (cc - ss) * pq + cs * (pp - qq)
    for r in range(order):
        if r != p and r != q:
            rp, rq = matrix[at(r, p)], matrix[at(r, q)]
            new[at(r, p)] = cosine * rp - sine * rq
            new[at(r, q)] = sine * rp + cosine * rq
    newv = dict(vectors)
    for r in range(order):
        vp, vq = vectors[r, p], vectors[r, q]
        newv[r, p] = cosine * vp - sine * vq
        newv[r, q] = sine * vp + cosine * vq
    return new, newv


def lowest(matrix, order):
    one = jnp.ones((1, LANES), f32)
    nil = jnp.zeros((1, LANES), f32)
    if order == 1:
        return matrix[0, 0], [one]
    keys = [(a, b) for a in range(order) for b in range(a, order)]
    vkeys = [(a, b) for a in range(order) for b in range(order)]

    def sweep(_, carry):
        m = dict(zip(keys, carry[: len(keys)]))
        v = dict(zip(vkeys, carry[len(keys) :]))
        for p in range(order):
            for q in range(p + 1, order):
                m, v = rotate(m, v, order, p, q)
        return tuple(m[x] for x in keys) + tuple(v[x] for x in vkeys)

    start = tuple(matrix[x] for x in keys) + tuple(one if a == b else nil for a, b in vkeys)
    out = lax.fori_loop(0, SWEEPS, sweep, start)
    m = dict(zip(keys, out[: len(keys)]))
    v = dict(zip(vkeys, out[len(keys) :]))
    theta = m[0, 0]
    weights = [v[r, 0] for r in range(order)]
    for j in range(1, order):
        less = m[j, j] < theta
        theta = jnp.where(less, m[j, j], theta)
        weights = [jnp.where(less, v[r, j], weights[r]) for r in range(order)]
    flip = weights[0] < 0.0
    return theta, [jnp.where(flip, -x, x) for x in weights]


PAIRS = [(a, b) for b in range(ITERS + 1) for a in range(b + 1)]
STATE_ROWS = 4 * len(PAIRS)


def load_state(state_ref, upto):
    state = {}
    for kind in range(4):
        for at, (a, b) in enumerate(PAIRS):
            if b < upto:
                row = kind * len(PAIRS) + at
                state[kind, a, b] = state_ref[row : row + 1, :]
    return state


def store_state(state_ref, state):
    for (kind, a, b), value in state.items():
        row = kind * len(PAIRS) + PAIRS.index((a, b))
        state_ref[row : row + 1, :] = value


def small_problem(count, sums, state):
    n = count - 1
    for a in range(n + 1):
        state[0, a, n] = sums[1 + a : 2 + a, :]
    for a in range(n):
        state[1, a, n] = sums[5 + a : 6 + a, :]
    state[1, n, n] = sums[0:1, :]
    gram = lambda a, b: state[0, min(a, b), max(a, b)]
    mixed = lambda a, b: state[1, min(a, b), max(a, b)]
    one = jnp.ones((1, LANES), f32)
    overlap = [sum(state[2, a, j] * gram(a, n) for a in range(j + 1)) for j in range(n)]
    raw = [-sum(overlap[j] * state[2, a, j] for j in range(a, n)) for a in range(n)] + [one]
    squared = sum(raw[a] * sum(raw[b] * gram(a, b) for b in range(n + 1)) for a in range(n + 1))
    scale = lax.rsqrt(jnp.maximum(squared, 0.0) + epsilon)
    for a in range(n + 1):
        state[2, a, n] = raw[a] * scale
    image = [sum(state[2, b, n] * mixed(a, b) for b in range(n + 1)) for a in range(n + 1)]
    for j in range(n + 1):
        state[3, j, n] = sum(state[2, a, j] * image[a] for a in range(j + 1))
    theta, weights = lowest(
        {(a, b): state[3, a, b] for a in range(count) for b in range(a, count)}, count
    )
    gammas = [sum(weights[j] * state[2, a, j] for j in range(a, count)) for a in range(count)]
    return theta, gammas


def lanes_of(shape):
    return lax.broadcasted_iota(jnp.int32, shape, len(shape) - 1)


def encode(values):
    high = values.astype(bf16).astype(f32)
    rest = values - high
    middle = rest.astype(bf16).astype(f32)
    low = rest - middle
    lane = lanes_of((8, LANES))
    parts = jnp.where(
        lane == 0, high, jnp.where(lane == 1, middle, jnp.where(lane == 2, low, 0.0))
    )
    return jnp.concatenate([parts, jnp.zeros((EXT - 8, LANES), f32)], axis=0).astype(bf16)


def decode(parts):
    return jnp.broadcast_to(jnp.sum(parts[0:8], axis=1, keepdims=True), (8, LANES))


def ext_sum(refs, first):
    total = None
    for ref, count in refs:
        part = ref[0, first : first + EXT, :].astype(f32)
        for b in range(1, count):
            part = part + ref[b, first : first + EXT, :].astype(f32)
        total = part if total is None else total + part
    return total


def scaled_sums(parts, total_count):
    row = lax.broadcasted_iota(jnp.int32, (8, LANES), 0)
    scale = jnp.where(row == 0, 0.5 / total_count, 0.5 / (N_RB * 2 * total_count))
    return decode(parts) * scale


def fold(x):
    return x.reshape(x.shape[0] // 8, 8, x.shape[1]).sum(axis=0)


def apply_kernel(count, total_count, *refs):
    refs = list(refs)
    place = refs.pop(0)
    left, folded = refs.pop(0), refs.pop(0)
    if count == 0:
        guess = [refs.pop(0) for _ in range(4)]
    else:
        diagonal = refs.pop(0)
        state_in = refs.pop(0) if count > 1 else None
        images = [[refs.pop(0) for _ in range(4)] for _ in range(count)]
        vectors = [refs.pop(0) for _ in range(count)]
    out, vector_out = refs.pop(0), refs.pop(0)
    if count > 0:
        state_out = refs.pop(0)
    x_ref, p_ref = refs

    lb, wa = place[0], place[1]
    if count > 0:
        newest = images[-1]
        sums = scaled_sums(
            ext_sum(((newest[0], N_RB), (newest[1], N_RB)), TILE), total_count
        )
        state = load_state(state_in, count - 1) if count > 1 else {}
        theta_row, gamma_rows = small_problem(count, sums, state)
        store_state(state_out, state)
        wide = lambda v: jnp.broadcast_to(v, (HALF, LANES))
        theta = wide(theta_row)
        gammas = [wide(g) for g in gamma_rows]
        deltas = [wide(-theta_row * g) for g in gamma_rows]

    def rows(s):
        return slice(s * HALF, (s + 1) * HALF)

    def cols(s):
        return slice(s * LANES, (s + 1) * LANES)

    n_sums = 1 if count == 0 else 2 * count + 1
    sums_at = tuple(jnp.zeros((8, LANES), f32) for _ in range(n_sums))
    for seg, (base, blocks, other) in enumerate(SEGMENTS):

        def body(b, acc, seg=seg, base=base, other=other):
            acc = list(acc)
            for s in range(S):
                if count == 0:
                    new = guess[seg][b, rows(s), :]
                    olds = []
                else:
                    olds = [v[base + b, rows(s), :].astype(f32) for v in vectors]
                    hs = [h[seg][b, rows(s), :].astype(f32) for h in images]
                    r = gammas[0] * hs[0] + deltas[0] * olds[0]
                    for i in range(1, count):
                        r = r + gammas[i] * hs[i] + deltas[i] * olds[i]
                    d = diagonal[base + b, rows(s), :]
                    new = (r / (jnp.abs(d - theta) + 1.0)).astype(bf16)
                vector_out[base + b, rows(s), :] = new
                if seg < 2:
                    at = pl.multiple_of(b * 2 * HALF + (wa ^ other) * HALF, HALF)
                    x_ref[pl.ds(at, HALF), cols(s)] = new
                    wide_new = new.astype(f32)
                    for i in range(count):
                        acc[i] = acc[i] + fold(olds[i] * wide_new)
                        acc[count + 1 + i] = acc[count + 1 + i] + fold(hs[i] * wide_new)
                    acc[count] = acc[count] + fold(wide_new * wide_new)
            return tuple(acc)

        sums_at = lax.fori_loop(0, blocks, body, sums_at)

    p_ref[...] = jnp.zeros_like(p_ref)

    def product(k, carry):
        y = jnp.dot(left[k], x_ref[...], preferred_element_type=f32).astype(bf16)
        p_ref[...] += jnp.dot(y, folded[k], preferred_element_type=f32)
        return carry

    lax.fori_loop(0, left.shape[0], product, 0)

    quad = jnp.zeros((8, LANES), f32)
    for base, blocks, other in SEGMENTS[2:]:

        def share(j, acc, base=base, other=other):
            rel = jnp.where(j < 4, j, 11 - j)
            at = pl.multiple_of((lb ^ rel) * 2 * HALF + (wa ^ other) * HALF, HALF)
            for s in range(S):
                new = vector_out[base + j, rows(s), :].astype(f32)
                acc = acc + fold(new * p_ref[pl.ds(at, HALF), cols(s)])
            return acc

        quad = lax.fori_loop(0, blocks, share, quad)

    values = [quad] + list(sums_at[: count + 1])
    places = list(range(count + 2))
    values += list(sums_at[count + 1 :])
    places += [5 + i for i in range(count)]
    row = lax.broadcasted_iota(jnp.int32, (8, LANES), 0)
    local = jnp.zeros((8, LANES), f32)
    for at, value in zip(places, values):
        one = jnp.sum(jnp.sum(value, axis=0, keepdims=True), axis=1, keepdims=True)
        local = jnp.where(row == at, jnp.broadcast_to(one, (8, LANES)), local)
    ext = encode(local)

    def write(t, carry):
        at = pl.multiple_of(t * HALF, HALF)
        for s in range(S):
            out[t, rows(s), :] = p_ref[pl.ds(at, HALF), cols(s)].astype(bf16)
        out[t, TILE:, :] = ext
        return carry

    lax.fori_loop(0, out.shape[0], write, 0)


def collect_kernel(parts, image, tile):
    count = parts.shape[0]
    for s in range(S):
        at = slice(s * HALF, (s + 1) * HALF)
        total = parts[0, at, :].astype(f32)
        for t in range(1, count):
            total = total + parts[t, at, :].astype(f32)
        image[at, :] = total
        tile[at, :] = total.astype(bf16)
    tile[TILE:, :] = encode(decode(ext_sum(((parts, count),), TILE)))


def finish_kernel(total_count, *refs):
    count = ITERS + 1
    exts, state_in = refs[0], refs[1]
    images = refs[2 : 2 + count]
    vectors = refs[2 + count : 2 + 2 * count]
    out = refs[-1]
    sums = scaled_sums(ext_sum(((exts, exts.shape[0]),), 0), total_count)
    state = load_state(state_in, count - 1)
    theta_row, gamma_rows = small_problem(count, sums, state)
    wide = lambda v: jnp.broadcast_to(v, (HALF, LANES))
    theta = wide(theta_row)
    gammas = [wide(g) for g in gamma_rows]
    for s in range(S):
        at = slice(s * HALF, (s + 1) * HALF)
        ritz = gammas[0] * vectors[0][0, at, :].astype(f32)
        residual = gammas[0] * images[0][at, :]
        for i in range(1, count):
            ritz = ritz + gammas[i] * vectors[i][0, at, :].astype(f32)
            residual = residual + gammas[i] * images[i][at, :]
        out[0, at, :] = ritz
        out[1, at, :] = residual - theta * ritz


VM = pl.BlockSpec(memory_space=pltpu.VMEM)
SM = pl.BlockSpec(memory_space=pltpu.SMEM)
shaped = jax.ShapeDtypeStruct


def apply(count, total_count, place, left, folded, others):
    outs = [
        shaped((2 * N_LB, TILE + EXT, LANES), bf16),
        shaped((BLOCKS, TILE, LANES), bf16),
    ]
    if count > 0:
        outs.append(shaped((STATE_ROWS, LANES), f32))
    rows_in, rows_out = left.shape[2], left.shape[1]
    width = S * LANES
    return pl.pallas_call(
        functools.partial(apply_kernel, count, total_count),
        out_shape=outs,
        in_specs=[SM] + [VM] * (2 + len(others)),
        out_specs=[VM] * len(outs),
        scratch_shapes=[pltpu.VMEM((rows_in, width), bf16), pltpu.VMEM((rows_out, width), f32)],
        compiler_params=pltpu.CompilerParams(vmem_limit_bytes=56 * 2**20),
        cost_estimate=pl.CostEstimate(
            flops=2 * left.shape[0] * rows_out * width * (rows_in + width),
            bytes_accessed=16 * 2**20,
            transcendentals=0,
        ),
        name=f"apply_{count}",
    )(place, left, folded, *others)


def collect(parts):
    return pl.pallas_call(
        collect_kernel,
        out_shape=[shaped((TILE, LANES), f32), shaped((TILE + EXT, LANES), bf16)],
        in_specs=[VM],
        out_specs=[VM, VM],
        name="collect",
    )(parts)


def finish(total_count, *others):
    return pl.pallas_call(
        functools.partial(finish_kernel, total_count),
        out_shape=shaped((2, TILE, LANES), f32),
        in_specs=[VM] * len(others),
        out_specs=VM,
        name="finish",
    )(*others)


def sent_to_all(x, axis):
    size = lax.axis_size(axis)
    return lax.all_to_all(jnp.broadcast_to(x[None], (size, *x.shape)), axis, 0, 0, tiled=True)


def swapped(x, axis, mask):
    size = lax.axis_size(axis)
    return lax.ppermute(x, axis, [(i, i ^ mask) for i in range(size)])


def gathered(tile):
    block_own = sent_to_all(tile, RB)
    along = tile[None]
    for mask in (1, 2, 7):
        along = jnp.concatenate([along, swapped(along, "lb", mask)], axis=0)
    along_other = swapped(along, "wa", 1)
    block_other = swapped(block_own, "wa", 1)
    return [block_own, block_other, along, along_other]


def dense_operator(operator_blocks, operator_pairs, levels):
    symmetric = 0.5 * (operator_blocks + jnp.swapaxes(operator_blocks, 1, 2))
    indices = jnp.arange(levels, dtype=jnp.int32)
    left_hot = (operator_pairs[:, 0:1] == indices[None, :]).astype(f32)
    right_hot = (operator_pairs[:, 1:2] == indices[None, :]).astype(f32)
    return jnp.einsum("nw,nv,nts->wvts", left_hot, right_hot, symmetric, precision=highest)


def per_device(initial_guess, left_environment, right_environment, operator_blocks, operator_pairs):
    own_rows, physical, window = initial_guess.shape
    levels = right_environment.shape[1]
    local_levels = left_environment.shape[0]
    block_rows = left_environment.shape[1] * left_environment.shape[3]
    contracted = left_environment.shape[4]
    total_count = float(
        own_rows * physical * window * lax.axis_size("lb") * lax.axis_size(RB)
    )
    lb = lax.axis_index("lb")
    rb = lax.axis_index(RB)
    wa = lax.axis_index("wa")
    place = jnp.stack([lb, wa]).astype(jnp.int32)
    left = left_environment.reshape(local_levels, block_rows, contracted)

    own_lines = lax.dynamic_slice_in_dim(left_environment, lb, 1, 1).reshape(
        local_levels, own_rows, contracted
    )
    line = lax.broadcasted_iota(jnp.int32, own_lines.shape, 1)
    column = lax.broadcasted_iota(jnp.int32, own_lines.shape, 2)
    left_diag = jnp.sum(
        jnp.where(column == line + rb * own_rows, own_lines.astype(f32), 0.0), axis=2
    ).astype(bf16)

    guess = lax.dynamic_slice_in_dim(
        jnp.swapaxes(initial_guess, 0, 1), wa * HALF, HALF, 1
    ).reshape(TILE, window)
    ext = jnp.pad(left_diag.reshape(-1, LANES), ((0, EXT - 2), (0, 0)))
    tiles = gathered(jnp.concatenate([guess, ext], axis=0))

    operator = dense_operator(operator_blocks, operator_pairs, levels)
    local_operator = lax.dynamic_slice_in_dim(operator, wa * local_levels, local_levels, 0)
    right_f = right_environment.astype(f32)
    folded = jnp.einsum("kvts,cvb->ksctb", local_operator, right_f, precision=highest)
    folded = folded.reshape(local_levels, physical * window, physical * window).astype(bf16)

    right_diag = jnp.diagonal(right_environment, axis1=0, axis2=2).astype(f32)
    by_level = jnp.einsum(
        "kvs,vb->ksb", jnp.diagonal(operator, axis1=2, axis2=3), right_diag, precision=highest
    )

    def levels_of(own, other):
        halves = [
            t[:, TILE : TILE + 2, :].astype(f32).reshape(-1, local_levels, 2, HALF)
            for t in (own, other)
        ]
        both = jnp.where(
            wa == 0, jnp.concatenate(halves, axis=1), jnp.concatenate(halves[::-1], axis=1)
        )
        first = jnp.where(wa == 0, both[:, :, 0], both[:, :, 1])
        second = jnp.where(wa == 0, both[:, :, 1], both[:, :, 0])
        return jnp.concatenate([first, second], axis=0)

    left_levels = jnp.concatenate(
        [levels_of(tiles[0], tiles[1]), levels_of(tiles[2], tiles[3])], axis=0
    )
    diagonal = jnp.einsum("nki,ksb->nsib", left_levels, by_level, precision=highest)
    diagonal = diagonal.reshape(BLOCKS, TILE, LANES)

    own_images, images, vectors = [], [], []
    state = None
    for count in range(ITERS + 1):
        if count == 0:
            others = tiles
        else:
            others = [diagonal] + ([state] if count > 1 else [])
            others += [t for h in images for t in h] + vectors
        result = apply(count, total_count, place, left, folded, others)
        vectors.append(result[1])
        if count > 0:
            state = result[2]
        arrived = lax.all_to_all(result[0], LB_WA, 0, 0, tiled=True)
        image, tile = collect(arrived)
        own_images.append(image)
        if count < ITERS:
            images.append(gathered(tile))
    exts = sent_to_all(tile[TILE:], RB_WA)
    own = 2 * N_RB
    out = finish(total_count, exts, state, *own_images, *[v[own : own + 1] for v in vectors])
    other = swapped(out, "wa", 1)
    pair = jnp.where(wa == 0, jnp.stack([out, other], 1), jnp.stack([other, out], 1))
    pair = pair.reshape(2, 2, physical, HALF, window)
    pair = jnp.transpose(pair, (0, 1, 3, 2, 4)).reshape(2, own_rows, physical, window)
    return (pair[0], pair[1])


def solution(mesh):
    split = Mesh(
        mesh.devices.reshape(mesh.shape["lb"], 4, 4, mesh.shape["wa"]), ("lb", "rb_0", "rb_1", "wa")
    )
    in_specs = (P(LB_RB, None, None), P("wa", None, RB, None, "lb"), P(), P(), P())
    out_specs = (P(LB_RB, None, None), P(LB_RB, None, None))
    return jax.shard_map(
        per_device, mesh=split, in_specs=in_specs, out_specs=out_specs, check_vma=False
    )
```

time: 928 us -> 329 us (0.35)
  blocking collectives: 367 us -> 69.8 us
  between operations: 186 us -> 1.06 us
  matrix products: 140 us -> 7.47 us
  Pallas kernels: 0 us -> 65.6 us
  other arithmetic: 69 us -> 12.8 us
  local copies, waits for them, and re-layouts: 83.2 us -> 37.6 us
  starting transfers between devices: 20.3 us -> 56.8 us
  waiting for transfers between devices: 56 us -> 73.3 us
    psum x24 -> x0, blocking collectives: 278 us -> none  [by_axis(): return functools.reduce(lax.psum, axes, x)]
    dot_general x14 -> x3, matrix products: 138 us -> 6.07 us  [the longest x1 3.25 us: per_device(): jnp.einsum('nki,ksb->nsib', left_levels, by_level, precision=highest)]
    pallas_call x0 -> x9, Pallas kernels: none -> 65.6 us  [the longest x4 54.8 us: apply(): pl.pallas_call(functools.partial(apply_kernel, count, total_count), out_s...]
    slice x85 -> x8, local copies, waits for them, and re-layouts: 56.7 us -> 7.69 us  [the longest x4 5.5 us: per_device(): v[own:own + 1]]
    ppermute x0 -> x21, waiting for transfers between devices: none -> 46.9 us  [swapped(): return lax.ppermute(x, axis, [(i, i ^ mask) for i in range(size)])]
    all_to_all x3 -> x1, waiting for transfers between devices: 47.7 us -> 13.9 us  [per_device(): arrived = lax.all_to_all(result[0], LB_WA, 0, 0, tiled=True)]
    ppermute x0 -> x21, starting transfers between devices: none -> 21.6 us  [swapped(): return lax.ppermute(x, axis, [(i, i ^ mask) for i in range(size)])]
    all_to_all x2 -> x5, starting transfers between devices: 9.38 us -> 30.9 us  [sent_to_all(): lax.all_to_all(jnp.broadcast_to(x[None], (size, *x.shape)), axis, 0, 0, t...]
  transfers between devices with their start and end apart: 5 -> 27, of which waited for: 4 -> 14; matrix products, arithmetic and copies ran while one was open for 2% -> 13% of each run, Pallas kernels for 0% -> 0%
where the time goes in v1:
time: 329 us; the launch traced here: 324 us
  waiting for transfers between devices  73.3 us (22%)
  blocking collectives  69.8 us (21%)
  Pallas kernels  65.6 us (20%)
  starting transfers between devices  56.8 us (17%)
  local copies, waits for them, and re-layouts  37.6 us (11%)
  other arithmetic  12.8 us (4%)
  matrix products  7.47 us (2%)
    all_to_all x3, blocking collectives, per_device(): arrived = lax.all_to_all(result[0], LB_WA, 0, 0, tiled=True)  69.8 us
    pallas_call x4, Pallas kernels, apply(): pl.pallas_call(functools.partial(apply_kernel, count, total_count), out_s...  54.8 us
    ppermute x21, waiting for transfers between devices, swapped(): return lax.ppermute(x, axis, [(i, i ^ mask) for i in range(size)])  46.9 us
    all_to_all x5, starting transfers between devices, sent_to_all(): lax.all_to_all(jnp.broadcast_to(x[None], (size, *x.shape)), axis, 0, 0, t...  30.9 us
    ppermute x21, starting transfers between devices, swapped(): return lax.ppermute(x, axis, [(i, i ^ mask) for i in range(size)])  21.6 us
    all_to_all x1, waiting for transfers between devices, per_device(): arrived = lax.all_to_all(result[0], LB_WA, 0, 0, tiled=True)  13.9 us
    all_to_all x5, waiting for transfers between devices, sent_to_all(): lax.all_to_all(jnp.broadcast_to(x[None], (size, *x.shape)), axis, 0, 0, t...  12.5 us
    unnamed x41, local copies, waits for them, and re-layouts  8.94 us
  transfers between devices with their start and end apart: 27, of which 14 were waited for; matrix products, arithmetic and copies ran while one was open for 13% of the time, Pallas kernels for 0%

profile of v1, /device:TPU:8, one launch (start us, length us, event | category | flops | bytes accessed | tf_op | source)
XLA Modules:
  0.0 324.5 jit_solution(3862781110188236721)
XLA Ops:
  5.9 7.4 %all-to-all-start = ((bf16[16,144,128]{2,1,0:T(8,128)(2,1)}), bf16[16,144,128]{2,1,0:T(8,128)(2,1)S(1)}, u32[]{:S(2)}, u32[]{:S(2)}) async-start(bf16[16,144,128]{2,1,0:T(8,128)(2,1)} %broadcast_in_dim.31), calls=%async_computation | async-start | bytes 1179648 | tf_op jit(solution)/shard_map/all_to_all | solution.py:382
  15.5 3.4 %collective-permute-start.2 = (bf16[2,144,128]{2,1,0:T(8,128)(2,1)S(1)}, bf16[2,144,128]{2,1,0:T(8,128)(2,1)S(1)}, u32[]{:S(2)}, u32[]{:S(2)}) collective-permute-start(bf16[2,144,128]{2,1,0:T(8,128)(2,1)S(1)} %pad_maximum_fusion.8), channel_id=1, source_target_pairs={{0,64},{32,96},{64,0},{96,32},{128,192},{160,224},{192,128},{224,1... | collective-permute-start | bytes 221192 | tf_op jit(solution)/shard_map/ppermute | solution.py:387
  21.6 5.2 %collective-permute-start.3 = (bf16[4,144,128]{2,1,0:T(8,128)(2,1)S(1)}, bf16[4,144,128]{2,1,0:T(8,128)(2,1)S(1)}, u32[]{:S(2)}, u32[]{:S(2)}) collective-permute-start(bf16[4,144,128]{2,1,0:T(8,128)(2,1)S(1)} %pad_maximum_fusion.4), channel_id=1, source_target_pairs={{0,224},{32,192},{64,160},{96,128},{128,96},{160,64},{192,32},{224... | collective-permute-start | bytes 442376 | tf_op jit(solution)/shard_map/ppermute | solution.py:387
  26.8 2.7 convert_bitcast_fusion
  29.5 3.2 copy.64
  32.7 3.0 copy.62
  35.7 4.1 %convert_element_type.32.refs_2_ = bf16[4,512,512]{2,1,0:T(8,128)(2,1)} reshape(bf16[4,4,128,4,128]{4,3,2,1,0:T(4,128)(2,1)} %copy.62) | data formatting | bytes 4194304 | tf_op jit(solution)/shard_map/convert_element_type | solution.py:442
  44.4 9.7 %apply_0.1 = (bf16[16,144,128]{2,1,0:T(8,128)(2,1)}, bf16[48,128,128]{2,1,0:T(8,128)(2,1)}) custom-call(s32[2]{0:T(128)} %pad_add_fusion.refs_0_, bf16[4,512,1024]{2,1,0:T(8,128)(2,1)} %bitcast.85, bf16[4,512,512]{2,1,0:T(8,128)(2,1)} %convert_element_type.32.refs_2_, bf16[16,144,128]{2,1,0:T(8,128)(2,1)} %copy-done.13, ...), custom_call_target="tpu_custom_call" | custom-call | flops 3221225472 | bytes 16777216 | tf_op jit(solution)/shard_map/apply_0/pallas_call | solution.py:344
  54.1 4.3 %all-to-all-start.1 = ((bf16[16,144,128]{2,1,0:T(8,128)(2,1)}), bf16[16,144,128]{2,1,0:T(8,128)(2,1)S(1)}, u32[]{:S(2)}, u32[]{:S(2)}) async-start(bf16[16,144,128]{2,1,0:T(8,128)(2,1)} %get-tuple-element.21), calls=%async_computation.1 | async-start | bytes 1179648 | tf_op jit(solution)/shard_map/all_to_all | solution.py:479
  61.7 13.9 %all-to-all-done.1.parts = bf16[16,144,128]{2,1,0:T(8,128)(2,1)S(1)} async-done(((bf16[16,144,128]{2,1,0:T(8,128)(2,1)}), bf16[16,144,128]{2,1,0:T(8,128)(2,1)S(1)}, u32[]{:S(2)}, u32[]{:S(2)}) %all-to-all-start.1) | async-done | bytes 589856 | tf_op jit(solution)/shard_map/all_to_all | solution.py:479
  80.2 6.4 %all-to-all-start.2 = ((bf16[16,144,128]{2,1,0:T(8,128)(2,1)}), bf16[16,144,128]{2,1,0:T(8,128)(2,1)S(1)}, u32[]{:S(2)}, u32[]{:S(2)}) async-start(bf16[16,144,128]{2,1,0:T(8,128)(2,1)} %broadcast_in_dim.33), calls=%async_computation.2 | async-start | bytes 1179648 | tf_op jit(solution)/shard_map/all_to_all | solution.py:382
  88.3 3.4 %collective-permute-start.7 = (bf16[2,144,128]{2,1,0:T(8,128)(2,1)S(1)}, bf16[2,144,128]{2,1,0:T(8,128)(2,1)S(1)}, u32[]{:S(2)}, u32[]{:S(2)}) collective-permute-start(bf16[2,144,128]{2,1,0:T(8,128)(2,1)S(1)} %pad_maximum_fusion.9), channel_id=1, source_target_pairs={{0,64},{32,96},{64,0},{96,32},{128,192},{160,224},{192,128},{224,1... | collective-permute-start | bytes 221192 | tf_op jit(solution)/shard_map/ppermute | solution.py:387
  91.8 4.4 %collective-permute-done.7 = bf16[2,144,128]{2,1,0:T(8,128)(2,1)S(1)} collective-permute-done((bf16[2,144,128]{2,1,0:T(8,128)(2,1)S(1)}, bf16[2,144,128]{2,1,0:T(8,128)(2,1)S(1)}, u32[]{:S(2)}, u32[]{:S(2)}) %collective-permute-start.7) | collective-permute-done | bytes 73760 | tf_op jit(solution)/shard_map/ppermute | solution.py:387
  98.7 8.6 %collective-permute-done.8 = bf16[4,144,128]{2,1,0:T(8,128)(2,1)S(1)} collective-permute-done((bf16[4,144,128]{2,1,0:T(8,128)(2,1)S(1)}, bf16[4,144,128]{2,1,0:T(8,128)(2,1)S(1)}, u32[]{:S(2)}, u32[]{:S(2)}) %collective-permute-start.8) | collective-permute-done | bytes 147488 | tf_op jit(solution)/shard_map/ppermute | solution.py:387
  107.4 3.3 %convolution_bitcast_fusion = f32[48,4,32,128]{3,0,2,1:T(8,128)S(1)} fusion(f32[8,4,128,1]{2,0,3,1:T(8,128)S(1)} %convolution_bitcast_fusion.1, f32[8,8,32]{0,1,2:T(8,128)S(1)} %get-tuple-element.45, f32[8,8,32]{0,1,2:T(8,128)S(1)} %get-tuple-element.44, f32[16,8,32]{0,1,2:T(8,128)S(1)} %get-tuple-element.43, f32[16,8,32]{0,1,2:T(8,128)S(1)} %get-tuple-element.42), kind=kOutput, calls=%fused_computation.3 | convolution fusion | flops 75534336 | bytes 3211264 | tf_op jit(solution)/shard_map/nki,ksb->nsib/dot_general | solution.py:464
  110.7 2.6 copy.75
  114.2 12.5 %apply_1.1 = (bf16[16,144,128]{2,1,0:T(8,128)(2,1)}, bf16[48,128,128]{2,1,0:T(8,128)(2,1)}, f32[40,128]{1,0:T(8,128)}) custom-call(s32[2]{0:T(128)} %pad_add_fusion.refs_0_, bf16[4,512,1024]{2,1,0:T(8,128)(2,1)} %bitcast.86, bf16[4,512,512]{2,1,0:T(8,128)(2,1)} %convert_element_type.32.refs_2_, f32[48,128,128]{2,1,0:T(8,128)} %bitcast.82, ...), custom_call_target="tpu_custom_call" | custom-call | flops 3221225472 | bytes 16777216 | tf_op jit(solution)/shard_map/apply_1/pallas_call | solution.py:344
  126.7 23.3 %all_to_all.45.parts = bf16[16,144,128]{2,1,0:T(8,128)(2,1)} all-to-all(bf16[16,144,128]{2,1,0:T(8,128)(2,1)} %get-tuple-element.25), channel_id=1, replica_groups=mesh['lb'=8,'rb_0'=4,'rb_1'=4,'wa'=2] {'lb','wa'}, dimensions={0} | all-to-all | bytes 1179648 | tf_op jit(solution)/shard_map/all_to_all | solution.py:479
  153.5 7.2 %all-to-all-start.4 = ((bf16[16,144,128]{2,1,0:T(8,128)(2,1)}), bf16[16,144,128]{2,1,0:T(8,128)(2,1)S(1)}, u32[]{:S(2)}, u32[]{:S(2)}) async-start(bf16[16,144,128]{2,1,0:T(8,128)(2,1)} %broadcast_in_dim.35), calls=%async_computation.4 | async-start | bytes 1179648 | tf_op jit(solution)/shard_map/all_to_all | solution.py:382
  161.6 3.3 %collective-permute-done.11 = bf16[1,144,128]{2,1,0:T(8,128)(2,1)S(1)} collective-permute-done((bf16[1,144,128]{2,1,0:T(8,128)(2,1)}, bf16[1,144,128]{2,1,0:T(8,128)(2,1)S(1)}, u32[]{:S(2)}, u32[]{:S(2)}) %collective-permute-start.11) | collective-permute-done | bytes 36896 | tf_op jit(solution)/shard_map/ppermute | solution.py:387
  166.6 5.5 %all-to-all-done.4.refs_9_ = bf16[16,144,128]{2,1,0:T(8,128)(2,1)S(1)} async-done(((bf16[16,144,128]{2,1,0:T(8,128)(2,1)}), bf16[16,144,128]{2,1,0:T(8,128)(2,1)S(1)}, u32[]{:S(2)}, u32[]{:S(2)}) %all-to-all-start.4) | async-done | bytes 589856 | tf_op jit(solution)/shard_map/all_to_all | solution.py:382
  173.5 10.1 %collective-permute-done.13 = bf16[4,144,128]{2,1,0:T(8,128)(2,1)S(1)} collective-permute-done((bf16[4,144,128]{2,1,0:T(8,128)(2,1)S(1)}, bf16[4,144,128]{2,1,0:T(8,128)(2,1)S(1)}, u32[]{:S(2)}, u32[]{:S(2)}) %collective-permute-start.13) | collective-permute-done | bytes 147488 | tf_op jit(solution)/shard_map/ppermute | solution.py:387
  187.3 14.9 %apply_2.1 = (bf16[16,144,128]{2,1,0:T(8,128)(2,1)}, bf16[48,128,128]{2,1,0:T(8,128)(2,1)}, f32[40,128]{1,0:T(8,128)}) custom-call(s32[2]{0:T(128)} %pad_add_fusion.refs_0_, bf16[4,512,1024]{2,1,0:T(8,128)(2,1)} %bitcast.87, bf16[4,512,512]{2,1,0:T(8,128)(2,1)} %convert_element_type.32.refs_2_, f32[48,128,128]{2,1,0:T(8,128)} %bitcast.83, ...), custom_call_target="tpu_custom_call" | custom-call | flops 3221225472 | bytes 16777216 | tf_op jit(solution)/shard_map/apply_2/pallas_call | solution.py:344
  202.2 23.3 %all_to_all.46.parts = bf16[16,144,128]{2,1,0:T(8,128)(2,1)} all-to-all(bf16[16,144,128]{2,1,0:T(8,128)(2,1)} %get-tuple-element.29), channel_id=1, replica_groups=mesh['lb'=8,'rb_0'=4,'rb_1'=4,'wa'=2] {'lb','wa'}, dimensions={0} | all-to-all | bytes 1179648 | tf_op jit(solution)/shard_map/all_to_all | solution.py:479
  229.0 4.9 %all-to-all-start.6 = ((bf16[16,144,128]{2,1,0:T(8,128)(2,1)}), bf16[16,144,128]{2,1,0:T(8,128)(2,1)S(1)}, u32[]{:S(2)}, u32[]{:S(2)}) async-start(bf16[16,144,128]{2,1,0:T(8,128)(2,1)} %broadcast_in_dim.63), calls=%async_computation.6 | async-start | bytes 1179648 | tf_op jit(solution)/shard_map/all_to_all | solution.py:382
  234.8 3.3 %collective-permute-done.16 = bf16[1,144,128]{2,1,0:T(8,128)(2,1)S(1)} collective-permute-done((bf16[1,144,128]{2,1,0:T(8,128)(2,1)}, bf16[1,144,128]{2,1,0:T(8,128)(2,1)S(1)}, u32[]{:S(2)}, u32[]{:S(2)}) %collective-permute-start.16) | collective-permute-done | bytes 36896 | tf_op jit(solution)/shard_map/ppermute | solution.py:387
  239.7 5.9 %all-to-all-done.6.refs_13_ = bf16[16,144,128]{2,1,0:T(8,128)(2,1)S(1)} async-done(((bf16[16,144,128]{2,1,0:T(8,128)(2,1)}), bf16[16,144,128]{2,1,0:T(8,128)(2,1)S(1)}, u32[]{:S(2)}, u32[]{:S(2)}) %all-to-all-start.6) | async-done | bytes 589856 | tf_op jit(solution)/shard_map/all_to_all | solution.py:382
  247.0 10.2 %collective-permute-done.18 = bf16[4,144,128]{2,1,0:T(8,128)(2,1)S(1)} collective-permute-done((bf16[4,144,128]{2,1,0:T(8,128)(2,1)S(1)}, bf16[4,144,128]{2,1,0:T(8,128)(2,1)S(1)}, u32[]{:S(2)}, u32[]{:S(2)}) %collective-permute-start.18) | collective-permute-done | bytes 147488 | tf_op jit(solution)/shard_map/ppermute | solution.py:387
  260.5 17.6 %apply_3.1 = (bf16[16,144,128]{2,1,0:T(8,128)(2,1)}, bf16[48,128,128]{2,1,0:T(8,128)(2,1)}, f32[40,128]{1,0:T(8,128)}) custom-call(s32[2]{0:T(128)} %pad_add_fusion.refs_0_, bf16[4,512,1024]{2,1,0:T(8,128)(2,1)} %bitcast.88, bf16[4,512,512]{2,1,0:T(8,128)(2,1)} %convert_element_type.32.refs_2_, f32[48,128,128]{2,1,0:T(8,128)} %bitcast.84, ...), custom_call_target="tpu_custom_call" | custom-call | flops 3221225472 | bytes 16777216 | tf_op jit(solution)/shard_map/apply_3/pallas_call | solution.py:344
  278.1 23.3 %all_to_all.47.parts = bf16[16,144,128]{2,1,0:T(8,128)(2,1)} all-to-all(bf16[16,144,128]{2,1,0:T(8,128)(2,1)} %get-tuple-element.32), channel_id=1, replica_groups=mesh['lb'=8,'rb_0'=4,'rb_1'=4,'wa'=2] {'lb','wa'}, dimensions={0} | all-to-all | bytes 1179648 | tf_op jit(solution)/shard_map/all_to_all | solution.py:479
  304.6 5.0 %all-to-all-start.8 = ((bf16[32,16,128]{2,1,0:T(8,128)(2,1)}), bf16[32,16,128]{2,1,0:T(8,128)(2,1)S(1)}, u32[]{:S(2)}, u32[]{:S(2)}) async-start(bf16[32,16,128]{2,1,0:T(8,128)(2,1)} %broadcast_in_dim.65), calls=%async_computation.8 | async-start | bytes 262144 | tf_op jit(solution)/shard_map/all_to_all | solution.py:382
  316.9 3.5 %finish.1 = f32[2,128,128]{2,1,0:T(8,128)} custom-call(bf16[32,16,128]{2,1,0:T(8,128)(2,1)} %copy-done.16, f32[40,128]{1,0:T(8,128)} %get-tuple-element.34.refs_1_, f32[128,128]{1,0:T(8,128)} %get-tuple-element.35.refs_2_, f32[128,128]{1,0:T(8,128)} %get-tuple-element.36.refs_3_, f32[128,128]{1,0:T(8,128)} %get-tuple-element.37.refs_4_, ...), custom_call_target="tpu_custom_call" | custom-call | tf_op jit(solution)/shard_map/finish/pallas_call | solution.py:371
  (140 shorter events, 64.3 us)
Async XLA Ops:
  0.6 26.1 %copy-start.12 = (bf16[128,8,128]{2,1,0:T(8,128)(2,1)S(1)}, bf16[128,8,128]{2,1,0:T(8,128)(2,1)}, u32[]{:S(2)}) copy-start(bf16[128,8,128]{2,1,0:T(8,128)(2,1)} %param.7) | copy-start | bytes 786436
  2.9 12.5 %collective-permute-start.1 = (bf16[1,144,128]{2,1,0:T(8,128)(2,1)S(1)}, bf16[1,144,128]{2,1,0:T(8,128)(2,1)S(1)}, u32[]{:S(2)}, u32[]{:S(2)}) collective-permute-start(bf16[1,144,128]{2,1,0:T(8,128)(2,1)S(1)} %get-tuple-element.47), channel_id=1, source_target_pairs={{0,32},{32,0},{64,96},{96,64},{128,160},{160,128},{192,224},{224,1... | collective-permute-start | bytes 110600 | tf_op jit(solution)/shard_map/ppermute | solution.py:387
  5.9 20.9 %all-to-all-start = ((bf16[16,144,128]{2,1,0:T(8,128)(2,1)}), bf16[16,144,128]{2,1,0:T(8,128)(2,1)S(1)}, u32[]{:S(2)}, u32[]{:S(2)}) async-start(bf16[16,144,128]{2,1,0:T(8,128)(2,1)} %broadcast_in_dim.31), calls=%async_computation | async-start | bytes 1179648 | tf_op jit(solution)/shard_map/all_to_all | solution.py:382
  15.5 6.1 %collective-permute-start.2 = (bf16[2,144,128]{2,1,0:T(8,128)(2,1)S(1)}, bf16[2,144,128]{2,1,0:T(8,128)(2,1)S(1)}, u32[]{:S(2)}, u32[]{:S(2)}) collective-permute-start(bf16[2,144,128]{2,1,0:T(8,128)(2,1)S(1)} %pad_maximum_fusion.8), channel_id=1, source_target_pairs={{0,64},{32,96},{64,0},{96,32},{128,192},{160,224},{192,128},{224,1... | collective-permute-start | bytes 221192 | tf_op jit(solution)/shard_map/ppermute | solution.py:387
  21.6 18.3 %collective-permute-start.3 = (bf16[4,144,128]{2,1,0:T(8,128)(2,1)S(1)}, bf16[4,144,128]{2,1,0:T(8,128)(2,1)S(1)}, u32[]{:S(2)}, u32[]{:S(2)}) collective-permute-start(bf16[4,144,128]{2,1,0:T(8,128)(2,1)S(1)} %pad_maximum_fusion.4), channel_id=1, source_target_pairs={{0,224},{32,192},{64,160},{96,128},{128,96},{160,64},{192,32},{224... | collective-permute-start | bytes 442376 | tf_op jit(solution)/shard_map/ppermute | solution.py:387
  26.7 16.9 %collective-permute-start = (bf16[16,144,128]{2,1,0:T(8,128)(2,1)S(1)}, bf16[16,144,128]{2,1,0:T(8,128)(2,1)}, u32[]{:S(2)}, u32[]{:S(2)}) collective-permute-start(bf16[16,144,128]{2,1,0:T(8,128)(2,1)S(1)} %all-to-all-done.refs_3_), channel_id=1, source_target_pairs={{0,1},{1,0},{2,3},{3,2},{4,5},{5,4},{6,7},{7,6},{8,9},{9,8},{10,11... | collective-permute-start | bytes 1769480 | tf_op jit(solution)/shard_map/ppermute | solution.py:387
  39.9 3.7 %collective-permute-start.4 = (bf16[8,144,128]{2,1,0:T(8,128)(2,1)S(1)}, bf16[8,144,128]{2,1,0:T(8,128)(2,1)S(1)}, u32[]{:S(2)}, u32[]{:S(2)}) collective-permute-start(bf16[8,144,128]{2,1,0:T(8,128)(2,1)S(1)} %pad_maximum_fusion.refs_5_), channel_id=1, source_target_pairs={{0,1},{1,0},{2,3},{3,2},{4,5},{5,4},{6,7},{7,6},{8,9},{9,8},{10,11... | collective-permute-start | bytes 884744 | tf_op jit(solution)/shard_map/ppermute | solution.py:387
  54.1 21.4 %all-to-all-start.1 = ((bf16[16,144,128]{2,1,0:T(8,128)(2,1)}), bf16[16,144,128]{2,1,0:T(8,128)(2,1)S(1)}, u32[]{:S(2)}, u32[]{:S(2)}) async-start(bf16[16,144,128]{2,1,0:T(8,128)(2,1)} %get-tuple-element.21), calls=%async_computation.1 | async-start | bytes 1179648 | tf_op jit(solution)/shard_map/all_to_all | solution.py:479
  78.2 29.1 %copy-start.15 = (bf16[144,128]{1,0:T(8,128)(2,1)S(1)}, bf16[144,128]{1,0:T(8,128)(2,1)}, u32[]{:S(2)}) copy-start(bf16[144,128]{1,0:T(8,128)(2,1)} %get-tuple-element.22) | copy-start | bytes 110596
  78.2 9.3 %collective-permute-start.6 = (bf16[1,144,128]{2,1,0:T(8,128)(2,1)}, bf16[1,144,128]{2,1,0:T(8,128)(2,1)S(1)}, u32[]{:S(2)}, u32[]{:S(2)}) collective-permute-start(bf16[1,144,128]{2,1,0:T(8,128)(2,1)} %bitcast.90), channel_id=1, source_target_pairs={{0,32},{32,0},{64,96},{96,64},{128,160},{160,128},{192,224},{224,1... | collective-permute-start | bytes 110600 | tf_op jit(solution)/shard_map/ppermute | solution.py:387
  80.2 17.5 %all-to-all-start.2 = ((bf16[16,144,128]{2,1,0:T(8,128)(2,1)}), bf16[16,144,128]{2,1,0:T(8,128)(2,1)S(1)}, u32[]{:S(2)}, u32[]{:S(2)}) async-start(bf16[16,144,128]{2,1,0:T(8,128)(2,1)} %broadcast_in_dim.33), calls=%async_computation.2 | async-start | bytes 1179648 | tf_op jit(solution)/shard_map/all_to_all | solution.py:382
  88.3 7.9 %collective-permute-start.7 = (bf16[2,144,128]{2,1,0:T(8,128)(2,1)S(1)}, bf16[2,144,128]{2,1,0:T(8,128)(2,1)S(1)}, u32[]{:S(2)}, u32[]{:S(2)}) collective-permute-start(bf16[2,144,128]{2,1,0:T(8,128)(2,1)S(1)} %pad_maximum_fusion.9), channel_id=1, source_target_pairs={{0,64},{32,96},{64,0},{96,32},{128,192},{160,224},{192,128},{224,1... | collective-permute-start | bytes 221192 | tf_op jit(solution)/shard_map/ppermute | solution.py:387
  97.1 10.2 %collective-permute-start.8 = (bf16[4,144,128]{2,1,0:T(8,128)(2,1)S(1)}, bf16[4,144,128]{2,1,0:T(8,128)(2,1)S(1)}, u32[]{:S(2)}, u32[]{:S(2)}) collective-permute-start(bf16[4,144,128]{2,1,0:T(8,128)(2,1)S(1)} %pad_maximum_fusion.5), channel_id=1, source_target_pairs={{0,224},{32,192},{64,160},{96,128},{128,96},{160,64},{192,32},{224... | collective-permute-start | bytes 442376 | tf_op jit(solution)/shard_map/ppermute | solution.py:387
  97.7 15.6 %copy-start.1 = (bf16[16,144,128]{2,1,0:T(8,128)(2,1)}, bf16[16,144,128]{2,1,0:T(8,128)(2,1)S(1)}, u32[]{:S(2)}) copy-start(bf16[16,144,128]{2,1,0:T(8,128)(2,1)S(1)} %all-to-all-done.2.refs_4_.refs_5_) | copy-start | bytes 1769476
  97.7 15.6 %collective-permute-start.5 = (bf16[16,144,128]{2,1,0:T(8,128)(2,1)S(1)}, bf16[16,144,128]{2,1,0:T(8,128)(2,1)S(1)}, u32[]{:S(2)}, u32[]{:S(2)}) collective-permute-start(bf16[16,144,128]{2,1,0:T(8,128)(2,1)S(1)} %all-to-all-done.2.refs_4_.refs_5_), channel_id=1, source_target_pairs={{0,1},{1,0},{2,3},{3,2},{4,5},{5,4},{6,7},{7,6},{8,9},{9,8},{10,11... | collective-permute-start | bytes 1769480 | tf_op jit(solution)/shard_map/ppermute | solution.py:387
  107.3 6.0 %collective-permute-start.9 = (bf16[8,144,128]{2,1,0:T(8,128)(2,1)S(1)}, bf16[8,144,128]{2,1,0:T(8,128)(2,1)S(1)}, u32[]{:S(2)}, u32[]{:S(2)}) collective-permute-start(bf16[8,144,128]{2,1,0:T(8,128)(2,1)S(1)} %pad_maximum_fusion.1.refs_6_.refs_7_), channel_id=1, source_target_pairs={{0,1},{1,0},{2,3},{3,2},{4,5},{5,4},{6,7},{7,6},{8,9},{9,8},{10,11... | collective-permute-start | bytes 884744 | tf_op jit(solution)/shard_map/ppermute | solution.py:387
  153.5 18.6 %all-to-all-start.4 = ((bf16[16,144,128]{2,1,0:T(8,128)(2,1)}), bf16[16,144,128]{2,1,0:T(8,128)(2,1)S(1)}, u32[]{:S(2)}, u32[]{:S(2)}) async-start(bf16[16,144,128]{2,1,0:T(8,128)(2,1)} %broadcast_in_dim.35), calls=%async_computation.4 | async-start | bytes 1179648 | tf_op jit(solution)/shard_map/all_to_all | solution.py:382
  160.7 4.2 %collective-permute-start.11 = (bf16[1,144,128]{2,1,0:T(8,128)(2,1)}, bf16[1,144,128]{2,1,0:T(8,128)(2,1)S(1)}, u32[]{:S(2)}, u32[]{:S(2)}) collective-permute-start(bf16[1,144,128]{2,1,0:T(8,128)(2,1)} %bitcast.94), channel_id=1, source_target_pairs={{0,32},{32,0},{64,96},{96,64},{128,160},{160,128},{192,224},{224,1... | collective-permute-start | bytes 110600 | tf_op jit(solution)/shard_map/ppermute | solution.py:387
  165.7 6.4 %collective-permute-start.12 = (bf16[2,144,128]{2,1,0:T(8,128)(2,1)S(1)}, bf16[2,144,128]{2,1,0:T(8,128)(2,1)S(1)}, u32[]{:S(2)}, u32[]{:S(2)}) collective-permute-start(bf16[2,144,128]{2,1,0:T(8,128)(2,1)S(1)} %pad_maximum_fusion.10), channel_id=1, source_target_pairs={{0,64},{32,96},{64,0},{96,32},{128,192},{160,224},{192,128},{224,1... | collective-permute-start | bytes 221192 | tf_op jit(solution)/shard_map/ppermute | solution.py:387
  172.1 14.2 %copy-start.3 = (bf16[16,144,128]{2,1,0:T(8,128)(2,1)}, bf16[16,144,128]{2,1,0:T(8,128)(2,1)S(1)}, u32[]{:S(2)}) copy-start(bf16[16,144,128]{2,1,0:T(8,128)(2,1)S(1)} %all-to-all-done.4.refs_9_) | copy-start | bytes 1769476
  172.1 14.2 %collective-permute-start.10 = (bf16[16,144,128]{2,1,0:T(8,128)(2,1)S(1)}, bf16[16,144,128]{2,1,0:T(8,128)(2,1)S(1)}, u32[]{:S(2)}, u32[]{:S(2)}) collective-permute-start(bf16[16,144,128]{2,1,0:T(8,128)(2,1)S(1)} %all-to-all-done.4.refs_9_), channel_id=1, source_target_pairs={{0,1},{1,0},{2,3},{3,2},{4,5},{5,4},{6,7},{7,6},{8,9},{9,8},{10,11... | collective-permute-start | bytes 1769480 | tf_op jit(solution)/shard_map/ppermute | solution.py:387
  173.0 10.7 %collective-permute-start.13 = (bf16[4,144,128]{2,1,0:T(8,128)(2,1)S(1)}, bf16[4,144,128]{2,1,0:T(8,128)(2,1)S(1)}, u32[]{:S(2)}, u32[]{:S(2)}) collective-permute-start(bf16[4,144,128]{2,1,0:T(8,128)(2,1)S(1)} %pad_maximum_fusion.6), channel_id=1, source_target_pairs={{0,224},{32,192},{64,160},{96,128},{128,96},{160,64},{192,32},{224... | collective-permute-start | bytes 442376 | tf_op jit(solution)/shard_map/ppermute | solution.py:387
  184.5 1.9 collective-permute-start.14
  229.0 16.6 %all-to-all-start.6 = ((bf16[16,144,128]{2,1,0:T(8,128)(2,1)}), bf16[16,144,128]{2,1,0:T(8,128)(2,1)S(1)}, u32[]{:S(2)}, u32[]{:S(2)}) async-start(bf16[16,144,128]{2,1,0:T(8,128)(2,1)} %broadcast_in_dim.63), calls=%async_computation.6 | async-start | bytes 1179648 | tf_op jit(solution)/shard_map/all_to_all | solution.py:382
  233.9 4.2 %collective-permute-start.16 = (bf16[1,144,128]{2,1,0:T(8,128)(2,1)}, bf16[1,144,128]{2,1,0:T(8,128)(2,1)S(1)}, u32[]{:S(2)}, u32[]{:S(2)}) collective-permute-start(bf16[1,144,128]{2,1,0:T(8,128)(2,1)} %bitcast.98), channel_id=1, source_target_pairs={{0,32},{32,0},{64,96},{96,64},{128,160},{160,128},{192,224},{224,1... | collective-permute-start | bytes 110600 | tf_op jit(solution)/shard_map/ppermute | solution.py:387
  238.8 6.8 %collective-permute-start.17 = (bf16[2,144,128]{2,1,0:T(8,128)(2,1)S(1)}, bf16[2,144,128]{2,1,0:T(8,128)(2,1)S(1)}, u32[]{:S(2)}, u32[]{:S(2)}) collective-permute-start(bf16[2,144,128]{2,1,0:T(8,128)(2,1)S(1)} %pad_maximum_fusion.11), channel_id=1, source_target_pairs={{0,64},{32,96},{64,0},{96,32},{128,192},{160,224},{192,128},{224,1... | collective-permute-start | bytes 221192 | tf_op jit(solution)/shard_map/ppermute | solution.py:387
  245.6 14.0 %copy-start.8 = (bf16[16,144,128]{2,1,0:T(8,128)(2,1)}, bf16[16,144,128]{2,1,0:T(8,128)(2,1)S(1)}, u32[]{:S(2)}) copy-start(bf16[16,144,128]{2,1,0:T(8,128)(2,1)S(1)} %all-to-all-done.6.refs_13_) | copy-start | bytes 1769476
  245.6 14.0 %collective-permute-start.15 = (bf16[16,144,128]{2,1,0:T(8,128)(2,1)S(1)}, bf16[16,144,128]{2,1,0:T(8,128)(2,1)S(1)}, u32[]{:S(2)}, u32[]{:S(2)}) collective-permute-start(bf16[16,144,128]{2,1,0:T(8,128)(2,1)S(1)} %all-to-all-done.6.refs_13_), channel_id=1, source_target_pairs={{0,1},{1,0},{2,3},{3,2},{4,5},{5,4},{6,7},{7,6},{8,9},{9,8},{10,11... | collective-permute-start | bytes 1769480 | tf_op jit(solution)/shard_map/ppermute | solution.py:387
  246.5 10.7 %collective-permute-start.18 = (bf16[4,144,128]{2,1,0:T(8,128)(2,1)S(1)}, bf16[4,144,128]{2,1,0:T(8,128)(2,1)S(1)}, u32[]{:S(2)}, u32[]{:S(2)}) collective-permute-start(bf16[4,144,128]{2,1,0:T(8,128)(2,1)S(1)} %pad_maximum_fusion.7), channel_id=1, source_target_pairs={{0,224},{32,192},{64,160},{96,128},{128,96},{160,64},{192,32},{224... | collective-permute-start | bytes 442376 | tf_op jit(solution)/shard_map/ppermute | solution.py:387
  257.9 1.7 collective-permute-start.19
  304.6 11.7 %all-to-all-start.8 = ((bf16[32,16,128]{2,1,0:T(8,128)(2,1)}), bf16[32,16,128]{2,1,0:T(8,128)(2,1)S(1)}, u32[]{:S(2)}, u32[]{:S(2)}) async-start(bf16[32,16,128]{2,1,0:T(8,128)(2,1)} %broadcast_in_dim.65), calls=%async_computation.8 | async-start | bytes 262144 | tf_op jit(solution)/shard_map/all_to_all | solution.py:382
  320.4 1.6 collective-permute-start.20
  (15 other events, 27.2 us)
